TPU v7x, 32 devices: a whole 2x2x4 slice. The times are simulated.
32 devices in a mesh: row: 8 (over z, y), col: 4 (over x, core).
Axes of the slice: x: 2, y: 2, z: 4, core: 2. Of those that a mesh axis runs over, the one named last changes fastest.
Arguments:
- tokens: bfloat16 [4096, 4096], P('row', 'col'), may hold values from -6 to 6
- norm_gain: bfloat16 [4096], P('col'), may hold values from 0.099609375 to 1.8984375
- gate_weight: bfloat16 [4096, 10240], P('row', 'col'), may hold values from -0.09375 to 0.09375
- linear_weight: bfloat16 [4096, 10240], P('row', 'col'), may hold values from -0.09375 to 0.09375
- output_weight: bfloat16 [10240, 4096], P('col', 'row'), may hold values from -0.078125 to 0.078125
Outputs:
- block_out: bfloat16 [4096, 4096], P('row', 'col')
All inputs are finite; a program needn't handle non-finite values.
Results may differ from a plain program's by a relative error of at most 0.0065.
Values may be sent and summed in bfloat16 or wider, within the bound.
A program may use at most 128 MiB of HBM per device.

v0:
```python
import functools

import jax
import jax.numpy as jnp
from jax import lax
from jax.experimental import pallas as pl
from jax.experimental.pallas import tpu as pltpu
from jax.sharding import PartitionSpec as P

LANES = 128
VMEM_LIMIT = 67043328
SCRATCH_MOST = 61 << 20
MESH = pl.DeviceIdType.MESH
F32 = jnp.float32
BF16 = jnp.bfloat16


def gathered(tokens, norm_gain, gate_weight, linear_weight, output_weight):
    whole = lax.all_gather(tokens, "col", axis=1, tiled=True)
    gain_all = lax.all_gather(norm_gain, "col", axis=0, tiled=True)
    normed = rms_normed(whole, gain_all)
    gate = dot(normed, lax.all_gather(gate_weight, "row", axis=0, tiled=True))
    linear = dot(normed, lax.all_gather(linear_weight, "row", axis=0, tiled=True))
    hidden = (jax.nn.gelu(gate, approximate=True) * linear).astype(BF16)
    terms = dot(hidden, lax.all_gather(output_weight, "row", axis=1, tiled=True))
    return lax.psum_scatter(terms, "col", scatter_dimension=1, tiled=True).astype(BF16)


def dot(left, right):
    return jnp.dot(left, right, preferred_element_type=F32)


def rms_normed(whole, gain_all):
    values = whole.astype(F32)
    meansq = jnp.mean(values * values, axis=-1, keepdims=True)
    return (values * lax.rsqrt(meansq + 1e-06) * gain_all.astype(F32)).astype(BF16)


def pick(index, table):
    value = jnp.int32(table[0])
    for at in range(1, len(table)):
        value = jnp.where(index == at, jnp.int32(table[at]), value)
    return value


def body(zs, tokens, gain, gate_w, linear_w, out_w, out, xn, gl, acc, hid, wo, ss, *sems):
    (loc, ss_s, ss_r, t_r, t_zr, t_zl, t_x, t_c, t_d, g_z, g_y, g_zs, g_ys, w_z, w_zs, w_x, w_xs,
     w_y, w_ys, h_r, h_x, h_c, h_d, o_r, o_s, credit) = sems
    size, width = tokens.shape
    part = hid.shape[2] // zs
    outw = out_w.shape[1]
    features = width * zs
    row, col = lax.axis_index("row"), lax.axis_index("col")
    z, y = row // 2, row % 2
    x, core = col // 2, col % 2
    xcol = (1 - x) * 2 + core
    ccol = x * 2 + 1 - core
    dcol = (1 - x) * 2 + 1 - core
    near = [z, z + 1 - 2 * (z % 2), zs - 1 - z, (z + 2) % zs]
    at_x, at_c, at_d = (row, xcol), (row, ccol), (row, dcol)
    at_y = (z * 2 + 1 - y, col)

    def at_z(to):
        return (to * 2 + y, col)

    def copy(src, dst, send, recv, to):
        return pltpu.make_async_remote_copy(
            src_ref=src, dst_ref=dst, send_sem=send, recv_sem=recv, device_id=to, device_id_type=MESH
        )

    def arrived(ref, sem):
        copy(ref, ref, sem, sem, at_c).wait_recv()

    def left_here(ref, sem):
        copy(ref, ref, sem, sem, at_c).wait_send()

    def gl_at(zz, yy, i):
        return gl.at[zz, yy, :, pl.ds(i * part, part)]

    def wo_at(slab, block):
        return wo.at[slab, pl.ds(pl.multiple_of(block * part, 128), part), :]

    def hid_at(b, k):
        return hid.at[b, :, pl.ds(pl.multiple_of(k * part, 128), part)]

    def cols_of(w, to):
        return w.at[:, pl.ds(pl.multiple_of(to * part, 128), part)]

    own = xn.at[col, z]
    w_slab, w_block = jnp.where(z == col, y, 2), jnp.where(z == col, col, z)
    ins = [
        pltpu.make_async_copy(tokens, own, loc.at[0]),
        pltpu.make_async_copy(cols_of(gate_w, z), gl_at(z, y, 0), loc.at[1]),
        pltpu.make_async_copy(cols_of(linear_w, z), gl_at(z, y, 1), loc.at[2]),
        pltpu.make_async_copy(
            out_w.at[pl.ds(pl.multiple_of(z * part, 128), part), :], wo_at(w_slab, w_block), loc.at[3]
        ),
    ]
    for each in ins:
        each.start()

    barrier = pltpu.get_barrier_semaphore()
    peers = [at_z(near[1]), at_z(near[2]), at_z(near[3]), at_y, at_x, at_c, at_d]
    for peer in peers:
        pl.semaphore_signal(barrier, inc=1, device_id=peer, device_id_type=MESH)

    ins[0].wait()
    piece = 64

    @pl.loop(0, size // piece)
    def _(i):
        rows = pl.ds(pl.multiple_of(i * piece, piece), piece)
        values = xn[col, z, rows, :].astype(F32)
        sums = jnp.sum(values * values, axis=-1, keepdims=True)
        ss[col, rows, :] = jnp.broadcast_to(sums, (piece, LANES))

    pl.semaphore_wait(barrier, len(peers))

    def g_send(m, i):
        to = near[m]
        copy(
            cols_of((gate_w, linear_w)[i], to), gl_at(z, y, i), g_zs.at[m, i], g_z.at[z, i], at_z(to)
        ).start()

    def g_pass(m, i):
        ref = gl_at(near[m], y, i)
        copy(ref, ref, g_ys.at[m, i], g_y.at[near[m], i], at_y).start()

    def g_took(m, i):
        arrived(gl_at(near[m], y, i), g_z.at[near[m], i])
        g_pass(m, i)

    g_send(2, 0)
    for n, peer in enumerate((at_x, at_c, at_d)):
        copy(ss.at[col], ss.at[col], ss_s.at[n], ss_r.at[col], peer).start()
    ins[1].wait()
    g_pass(0, 0)
    ins[2].wait()
    g_pass(0, 1)
    for k in (xcol, ccol, dcol):
        arrived(ss.at[k], ss_r.at[k])

    @pl.loop(0, size // piece)
    def _(i):
        rows = pl.ds(pl.multiple_of(i * piece, piece), piece)
        total = ss[0, rows, :]
        for k in range(1, zs):
            total = total + ss[k, rows, :]
        scale = lax.rsqrt(total * (1.0 / features) + 1e-06)
        scale = jnp.concatenate([scale] * (width // LANES), axis=1)
        values = xn[col, z, rows, :].astype(F32) * scale * gain[...].astype(F32)
        xn[col, z, rows, :] = values.astype(BF16)

    def t_right(b):
        copy(xn.at[col, b], xn.at[col, b], t_zr.at[b], t_r.at[col, b], at_z(z + 1)).start()

    def t_left(b):
        copy(xn.at[col, b], xn.at[col, b], t_zl.at[b], t_r.at[col, b], at_z(z - 1)).start()

    def t_col(b):
        copy(xn.at[col, b], xn.at[col, b], t_x.at[b], t_r.at[col, b], at_x).start()
        copy(xn.at[col, b], xn.at[col, b], t_c.at[b], t_r.at[col, b], at_c).start()

    def t_over(b):
        arrived(xn.at[xcol, b], t_r.at[xcol, b])
        copy(xn.at[xcol, b], xn.at[xcol, b], t_d.at[b], t_r.at[xcol, b], at_c).start()

    pl.when(z < zs - 1)(lambda: t_right(z))
    pl.when(z > 0)(lambda: t_left(z))
    t_col(z)
    g_send(1, 0)
    g_send(1, 1)

    def w_out(m):
        zz = near[m]
        slab, block = jnp.where(zz == col, y, 2), jnp.where(zz == col, col, zz)
        ref = wo_at(slab, block)

        @pl.when(zz == col)
        def _():
            copy(ref, ref, w_ys.at[col], w_y.at[col], at_y).start()

        @pl.when(zz != col)
        def _():
            copy(ref, wo_at(y, col), w_xs.at[m], w_x.at[col], (row, zz)).start()

    def w_send(m):
        to = near[m]
        copy(
            out_w.at[pl.ds(pl.multiple_of(to * part, 128), part), :],
            wo_at(w_slab, w_block), w_zs.at[m], w_z.at[z], at_z(to),
        ).start()

    def w_took(m):
        zz = near[m]
        slab, block = jnp.where(zz == col, y, 2), jnp.where(zz == col, col, zz)
        arrived(wo_at(slab, block), w_z.at[zz])
        w_out(m)

    ins[3].wait()
    w_out(0)

    def t_step(s):
        @pl.when(z >= s)
        def _():
            b = z - s
            arrived(xn.at[col, b], t_r.at[col, b])
            pl.when(z < zs - 1)(lambda: t_right(b))
            t_col(b)

        @pl.when(z + s < zs)
        def _():
            b = z + s
            arrived(xn.at[col, b], t_r.at[col, b])
            pl.when(z > 0)(lambda: t_left(b))
            t_col(b)

    def t_over_step(s):
        pl.when(z >= s)(lambda: t_over(z - s))
        pl.when(z + s < zs)(lambda: t_over(z + s))

    t_step(1)
    g_send(2, 1)
    g_send(3, 0)
    t_over(z)
    t_step(2)
    g_send(3, 1)
    t_over_step(1)
    t_step(3)
    for m in (2, 3, 1):
        w_send(m)
    t_over_step(2)
    g_took(1, 0)
    g_took(1, 1)
    t_over_step(3)
    g_took(2, 0)

    tile = 2 * LANES
    tiles = 2 * part // tile
    depth = gl.shape[2]

    def product(kk, b, n):
        lanes = pl.ds(pl.multiple_of(n * tile, tile), tile)
        return dot(xn[kk, b, :, :depth], gl[kk, 0, :, lanes]) + dot(
            xn[kk, b, :, depth:], gl[kk, 1, :, lanes]
        ), lanes

    def inputs(m, first):
        kk = near[m]
        if first:
            for b in range(zs):
                for k in (ccol, dcol):
                    arrived(xn.at[k, b], t_r.at[k, b])
        for i in range(2):
            arrived(gl_at(kk, 1 - y, i), g_y.at[kk, i])

        @pl.loop(0, zs * tiles)
        def _(i):
            b, n = i // tiles, i % tiles
            value, lanes = product(kk, b, n)
            if first:
                acc[b, :, lanes] = value
            else:
                acc[b, :, lanes] = acc[b, :, lanes] + value

    inputs(0, True)
    g_took(2, 1)
    inputs(1, False)
    g_took(3, 0)
    g_took(3, 1)
    inputs(2, False)

    orders = [sorted(range(zs), key=lambda b, at=at: -abs(b - at)) for at in range(zs)]
    blocks = [pick(z, [order[j] for order in orders]) for j in range(zs)]

    last = near[3]
    for i in range(2):
        arrived(gl_at(last, 1 - y, i), g_y.at[last, i])
    cut = 64

    for j in range(zs):
        b = blocks[j]

        @pl.loop(0, tiles)
        def _(n, b=b):
            value, lanes = product(last, b, n)
            acc[b, :, lanes] = acc[b, :, lanes] + value

        @pl.loop(0, size // cut)
        def _(i, b=b):
            rows = pl.ds(pl.multiple_of(i * cut, cut), cut)
            gate = acc[b, rows, :part]
            linear = acc[b, rows, part:]
            value = (jax.nn.gelu(gate, approximate=True) * linear).astype(BF16)
            hid[b, rows, pl.ds(pl.multiple_of(col * part, 128), part)] = value

        copy(hid_at(b, col), hid_at(b, col), h_x.at[j], h_r.at[col, b], at_x).start()
        copy(hid_at(b, col), hid_at(b, col), h_c.at[j], h_r.at[col, b], at_c).start()

    def h_over(j):
        b = blocks[j]
        arrived(hid_at(b, xcol), h_r.at[xcol, b])
        copy(hid_at(b, xcol), hid_at(b, xcol), h_d.at[j], h_r.at[xcol, b], at_c).start()

    for b in range(zs):
        left_here(xn.at[col, b], t_x.at[b])
        left_here(xn.at[col, b], t_c.at[b])
        left_here(xn.at[xcol, b], t_d.at[b])

        @pl.when((b <= z) & (z < zs - 1))
        def _(b=b):
            left_here(xn.at[col, b], t_zr.at[b])

        @pl.when((b >= z) & (z > 0))
        def _(b=b):
            left_here(xn.at[col, b], t_zl.at[b])

    @pl.when(z > 0)
    def _():
        pl.semaphore_signal(credit.at[0], inc=1, device_id=at_z(z - 1), device_id_type=MESH)

    @pl.when(z < zs - 1)
    def _():
        pl.semaphore_signal(credit.at[1], inc=1, device_id=at_z(z + 1), device_id_type=MESH)

    h_over(0)
    w_took(2)
    w_took(3)
    h_over(1)
    w_took(1)

    def w_over(p):
        arrived(wo_at(y, p), w_x.at[p])
        copy(wo_at(y, p), wo_at(y, p), w_ys.at[p], w_y.at[p], at_y).start()

    w_over(ccol)
    w_over(xcol)
    w_over(dcol)
    pl.when(z < zs - 1)(lambda: pl.semaphore_wait(credit.at[0], 1))
    pl.when(z > 0)(lambda: pl.semaphore_wait(credit.at[1], 1))
    h_over(2)
    h_over(3)
    for p in range(zs):
        arrived(wo_at(1 - y, p), w_y.at[p])

    wide = 2 * LANES
    half = outw // wide
    for j in range(zs):
        b = blocks[j]
        for k in (ccol, dcol):
            arrived(hid_at(b, k), h_r.at[k, b])
        from_left = (b >= z) & (z > 0)
        from_right = (b <= z) & (z < zs - 1)

        @pl.when(from_left)
        def _(b=b):
            arrived(xn.at[0, b], o_r.at[0, b])

        @pl.when(from_right)
        def _(b=b):
            slot = jnp.where(b == z, 2, 0)
            arrived(xn.at[slot, b], o_r.at[1, b])

        @pl.loop(0, 2 * half)
        def _(n, b=b, j=j, from_left=from_left, from_right=from_right):
            yy, at = n // half, n % half
            value = dot(hid[b], wo[yy, :, pl.ds(pl.multiple_of(at * wide, wide), wide)])
            lanes = pl.ds(pl.multiple_of(n * wide, wide), wide)
            if j < zs - 1:
                carried = xn[0, b, :, lanes].astype(F32)
                value = value + jnp.where(from_left | from_right, carried, 0.0)
                xn[1, b, :, lanes] = value.astype(BF16)
            else:
                value = value + jnp.where(from_left, xn[0, b, :, lanes].astype(F32), 0.0)
                value = value + jnp.where(from_right, xn[2, b, :, lanes].astype(F32), 0.0)
                out[:, lanes] = value.astype(BF16)

        if j < zs - 1:

            @pl.when(b > z)
            def _(b=b, j=j):
                copy(xn.at[1, b], xn.at[0, b], o_s.at[j], o_r.at[0, b], at_z(z + 1)).start()

            @pl.when(b < z)
            def _(b=b, j=j):
                slot = jnp.where(b == z - 1, 2, 0)
                copy(xn.at[1, b], xn.at[slot, b], o_s.at[j], o_r.at[1, b], at_z(z - 1)).start()

    for n in range(3):
        left_here(ss.at[col], ss_s.at[n])
    for m in range(zs):
        for i in range(2):
            if m:
                left_here(gl_at(z, y, i), g_zs.at[m, i])
            left_here(gl_at(near[m], y, i), g_ys.at[m, i])
        if m:
            left_here(wo_at(w_slab, w_block), w_zs.at[m])
        pl.when(near[m] != col)(lambda m=m: left_here(wo_at(y, col), w_xs.at[m]))
        left_here(wo_at(y, m), w_ys.at[m])
    for j in range(zs):
        left_here(hid_at(blocks[j], col), h_x.at[j])
        left_here(hid_at(blocks[j], col), h_c.at[j])
        left_here(hid_at(blocks[j], xcol), h_d.at[j])
        if j < zs - 1:
            left_here(xn.at[1, blocks[j]], o_s.at[j])


def scratch_of(zs, size, width, depth, part, outw):
    cols = zs
    dma = pltpu.SemaphoreType.DMA
    buffers = [
        ((cols, zs, size, width), BF16),
        ((zs, 2, depth, 2 * part), BF16),
        ((zs, size, 2 * part), F32),
        ((zs, size, cols * part), BF16),
        ((3, cols * part, outw), BF16),
        ((cols, size, LANES), F32),
    ]
    sems = [
        (4,), (3,), (cols,), (cols, zs), (zs,), (zs,), (zs,), (zs,), (zs,), (zs, 2), (zs, 2), (zs, 2), (zs, 2),
        (zs,), (zs,), (cols,), (zs,), (cols,), (cols,), (cols, zs), (zs,), (zs,), (zs,), (2, zs), (zs,),
    ]
    return buffers, [dma(s) for s in sems] + [pltpu.SemaphoreType.REGULAR((2,))]


def fused(zs, buffers, sems, tokens, norm_gain, gate_weight, linear_weight, output_weight):
    anywhere = pl.BlockSpec(memory_space=pl.ANY)
    vmem = pl.BlockSpec(memory_space=pltpu.VMEM)
    return pl.pallas_call(
        functools.partial(body, zs),
        out_shape=jax.ShapeDtypeStruct(tokens.shape, BF16),
        in_specs=[anywhere, vmem, anywhere, anywhere, anywhere],
        out_specs=vmem,
        scratch_shapes=[pltpu.VMEM(shape, kind) for shape, kind in buffers] + sems,
        compiler_params=pltpu.CompilerParams(
            collective_id=0, has_side_effects=True, vmem_limit_bytes=VMEM_LIMIT
        ),
        name="ffn",
    )(tokens, norm_gain.reshape(1, -1), gate_weight, linear_weight, output_weight)


def solution(mesh):
    rows, cols = mesh.shape["row"], mesh.shape["col"]
    zs, xs = rows // 2, cols // 2

    def local(tokens, norm_gain, gate_weight, linear_weight, output_weight):
        args = (tokens, norm_gain, gate_weight, linear_weight, output_weight)
        size, width = tokens.shape
        depth, units = gate_weight.shape
        outw = output_weight.shape[1]
        part = units // zs
        fits = xs == 2 and zs == cols == 4 and units % (zs * LANES) == 0
        fits = fits and 2 * depth == width and 2 * outw == width and outw % (2 * LANES) == 0
        fits = fits and size % 64 == 0
        if fits:
            buffers, sems = scratch_of(zs, size, width, depth, part, outw)
            held = sum(functools.reduce(lambda a, b: a * b, s) * jnp.dtype(k).itemsize for s, k in buffers)
            if held <= SCRATCH_MOST:
                return fused(zs, buffers, sems, *args)
        return gathered(*args)

    return jax.shard_map(
        local,
        mesh=mesh,
        in_specs=(P("row", "col"), P("col"), P("row", "col"), P("row", "col"), P("col", "row")),
        out_specs=P("row", "col"),
        check_vma=False,
    )
```

profile of v0, /device:TPU:20, one launch (start us, length us, event | category | flops | bytes accessed | tf_op | source)
XLA Modules:
  0.0 407.6 jit_solution(4069300453708791775)
XLA Ops:
  0.0 1.3 reshape.3.gain
  1.3 404.1 %ffn.1 = bf16[512,1024]{1,0:T(8,128)(2,1)} custom-call(bf16[512,1024]{1,0:T(8,128)(2,1)} %tokens.1, bf16[1,1024]{1,0:T(2,128)(2,1)} %reshape.3.gain, bf16[512,2560]{1,0:T(8,128)(2,1)} %gate_w.1, bf16[512,2560]{1,0:T(8,128)(2,1)} %linear_w.1, bf16[2560,512]{1,0:T(8,128)(2,1)} %out_w.1), custom_call_target="tpu_custom_call" | custom-call | tf_op jit(solution)/shard_map/ffn/pallas_call | solution.py:429
  405.4 2.3 copy.7
where the time goes:
time: 408 us
  Pallas kernels  404 us (99%)
    pallas_call x1, Pallas kernels, fused(): pl.pallas_call(functools.partial(body, zs), out_shape=jax.ShapeDtypeStruc...  404 us

commit v1 on v0

--- a/solution.py
+++ b/solution.py
@@ -50,6 +50,7 @@
     part = hid.shape[2] // zs
     outw = out_w.shape[1]
     features = width * zs
+    wide = outw // 2
     row, col = lax.axis_index("row"), lax.axis_index("col")
     z, y = row // 2, row % 2
     x, core = col // 2, col % 2
@@ -57,6 +58,8 @@
     ccol = x * 2 + 1 - core
     dcol = (1 - x) * 2 + 1 - core
     near = [z, z + 1 - 2 * (z % 2), zs - 1 - z, (z + 2) % zs]
+    inner = (z > 0) & (z < zs - 1)
+    outer = jnp.logical_not(inner)
     at_x, at_c, at_d = (row, xcol), (row, ccol), (row, dcol)
     at_y = (z * 2 + 1 - y, col)
 
@@ -77,8 +80,12 @@
     def gl_at(zz, yy, i):
         return gl.at[zz, yy, :, pl.ds(i * part, part)]
 
-    def wo_at(slab, block):
-        return wo.at[slab, pl.ds(pl.multiple_of(block * part, 128), part), :]
+    def wo_at(slab, block, h):
+        rows = pl.ds(pl.multiple_of(block * part, 128), part)
+        return wo.at[slab, rows, pl.ds(h * wide, wide)]
+
+    def out_rows(to, h):
+        return out_w.at[pl.ds(pl.multiple_of(to * part, 128), part), pl.ds(h * wide, wide)]
 
     def hid_at(b, k):
         return hid.at[b, :, pl.ds(pl.multiple_of(k * part, 128), part)]
@@ -92,9 +99,8 @@
         pltpu.make_async_copy(tokens, own, loc.at[0]),
         pltpu.make_async_copy(cols_of(gate_w, z), gl_at(z, y, 0), loc.at[1]),
         pltpu.make_async_copy(cols_of(linear_w, z), gl_at(z, y, 1), loc.at[2]),
-        pltpu.make_async_copy(
-            out_w.at[pl.ds(pl.multiple_of(z * part, 128), part), :], wo_at(w_slab, w_block), loc.at[3]
-        ),
+        pltpu.make_async_copy(out_rows(z, 0), wo_at(w_slab, w_block, 0), loc.at[3]),
+        pltpu.make_async_copy(out_rows(z, 1), wo_at(w_slab, w_block, 1), loc.at[4]),
     ]
     for each in ins:
         each.start()
@@ -122,21 +128,22 @@
             cols_of((gate_w, linear_w)[i], to), gl_at(z, y, i), g_zs.at[m, i], g_z.at[z, i], at_z(to)
         ).start()
 
-    def g_pass(m, i):
-        ref = gl_at(near[m], y, i)
-        copy(ref, ref, g_ys.at[m, i], g_y.at[near[m], i], at_y).start()
-
-    def g_took(m, i):
-        arrived(gl_at(near[m], y, i), g_z.at[near[m], i])
-        g_pass(m, i)
-
-    g_send(2, 0)
+    def g_pass(zz, i):
+        ref = gl_at(zz, y, i)
+        copy(ref, ref, g_ys.at[zz, i], g_y.at[zz, i], at_y).start()
+
+    def g_took(zz, i):
+        arrived(gl_at(zz, y, i), g_z.at[zz, i])
+        g_pass(zz, i)
+
+    g_send(1, 0)
+    pl.when(inner)(lambda: g_send(2, 0))
     for n, peer in enumerate((at_x, at_c, at_d)):
         copy(ss.at[col], ss.at[col], ss_s.at[n], ss_r.at[col], peer).start()
     ins[1].wait()
-    g_pass(0, 0)
+    g_pass(z, 0)
     ins[2].wait()
-    g_pass(0, 1)
+    g_pass(z, 1)
     for k in (xcol, ccol, dcol):
         arrived(ss.at[k], ss_r.at[k])
 
@@ -165,40 +172,32 @@
         arrived(xn.at[xcol, b], t_r.at[xcol, b])
         copy(xn.at[xcol, b], xn.at[xcol, b], t_d.at[b], t_r.at[xcol, b], at_c).start()
 
-    pl.when(z < zs - 1)(lambda: t_right(z))
-    pl.when(z > 0)(lambda: t_left(z))
-    t_col(z)
-    g_send(1, 0)
-    g_send(1, 1)
-
-    def w_out(m):
+    def w_place(zz):
+        return jnp.where(zz == col, y, 2), jnp.where(zz == col, col, zz)
+
+    def w_out(m, h):
         zz = near[m]
-        slab, block = jnp.where(zz == col, y, 2), jnp.where(zz == col, col, zz)
-        ref = wo_at(slab, block)
+        ref = wo_at(*w_place(zz), h)
 
         @pl.when(zz == col)
         def _():
-            copy(ref, ref, w_ys.at[col], w_y.at[col], at_y).start()
+            copy(ref, ref, w_ys.at[col, h], w_y.at[col, h], at_y).start()
 
         @pl.when(zz != col)
         def _():
-            copy(ref, wo_at(y, col), w_xs.at[m], w_x.at[col], (row, zz)).start()
-
-    def w_send(m):
+            copy(ref, wo_at(y, col, h), w_xs.at[m, h], w_x.at[col, h], (row, zz)).start()
+
+    def w_send(m, h):
         to = near[m]
-        copy(
-            out_w.at[pl.ds(pl.multiple_of(to * part, 128), part), :],
-            wo_at(w_slab, w_block), w_zs.at[m], w_z.at[z], at_z(to),
-        ).start()
-
-    def w_took(m):
-        zz = near[m]
-        slab, block = jnp.where(zz == col, y, 2), jnp.where(zz == col, col, zz)
-        arrived(wo_at(slab, block), w_z.at[zz])
-        w_out(m)
-
-    ins[3].wait()
-    w_out(0)
+        copy(out_rows(to, h), wo_at(w_slab, w_block, h), w_zs.at[m, h], w_z.at[z, h], at_z(to)).start()
+
+    def w_took(m, h):
+        arrived(wo_at(*w_place(near[m]), h), w_z.at[near[m], h])
+        w_out(m, h)
+
+    def w_over(p, h):
+        arrived(wo_at(y, p, h), w_x.at[p, h])
+        copy(wo_at(y, p, h), wo_at(y, p, h), w_ys.at[p, h], w_y.at[p, h], at_y).start()
 
     def t_step(s):
         @pl.when(z >= s)
@@ -219,71 +218,131 @@
         pl.when(z >= s)(lambda: t_over(z - s))
         pl.when(z + s < zs)(lambda: t_over(z + s))
 
+    far_inner, far_outer = ((2, 1), (3, 0), (3, 1)), ((3, 0), (3, 1), (2, 0), (2, 1))
+
+    def both(on_inner, on_outer):
+        pl.when(inner)(on_inner)
+        pl.when(outer)(on_outer)
+
+    def stage(k):
+        def on(pieces):
+            if 0 < k <= len(pieces):
+                left_here(gl_at(z, y, 0), g_zs.at[pieces[k - 1]])
+            if k < len(pieces):
+                g_send(*pieces[k])
+
+        both(lambda: on(far_inner), lambda: on(far_outer))
+
+    def w_stage(h):
+        if h:
+            for m in (2, 3):
+                left_here(wo_at(w_slab, w_block, 0), w_zs.at[m, 0])
+
+        def on(order):
+            for m in order:
+                w_send(m, h)
+
+        both(lambda: on((2, 3)), lambda: on((3, 2)))
+
+    pl.when(z < zs - 1)(lambda: t_right(z))
+    pl.when(z > 0)(lambda: t_left(z))
+    t_col(z)
+    pl.when(outer)(lambda: g_send(1, 1))
+    third = jnp.where(inner, near[2], near[3])
+    last = jnp.where(inner, near[3], near[2])
+    g_took(near[1], 0)
+    pl.when(inner)(lambda: g_took(third, 0))
     t_step(1)
-    g_send(2, 1)
-    g_send(3, 0)
+
+    pl.when(inner)(lambda: g_took(near[1], 1))
+    t_step(2)
+    stage(0)
+    pl.when(inner)(lambda: g_send(1, 1))
+    t_step(3)
     t_over(z)
-    t_step(2)
-    g_send(3, 1)
     t_over_step(1)
-    t_step(3)
-    for m in (2, 3, 1):
-        w_send(m)
+    stage(1)
+    for h in range(2):
+        w_send(1, h)
+
+    def on_inner():
+        g_took(third, 1)
+        g_took(last, 0)
+
+    both(on_inner, lambda: g_took(near[1], 1))
     t_over_step(2)
-    g_took(1, 0)
-    g_took(1, 1)
     t_over_step(3)
-    g_took(2, 0)
+    for h in range(2):
+        ins[3 + h].wait()
+        w_out(0, h)
 
     tile = 2 * LANES
     tiles = 2 * part // tile
     depth = gl.shape[2]
 
-    def product(kk, b, n):
+    def product(kk, b, n, yys):
         lanes = pl.ds(pl.multiple_of(n * tile, tile), tile)
-        return dot(xn[kk, b, :, :depth], gl[kk, 0, :, lanes]) + dot(
-            xn[kk, b, :, depth:], gl[kk, 1, :, lanes]
-        ), lanes
-
-    def inputs(m, first):
-        kk = near[m]
-        if first:
-            for b in range(zs):
-                for k in (ccol, dcol):
-                    arrived(xn.at[k, b], t_r.at[k, b])
-        for i in range(2):
-            arrived(gl_at(kk, 1 - y, i), g_y.at[kk, i])
-
+        value = None
+        for yy in yys:
+            columns = pl.ds(pl.multiple_of(yy * depth, depth), depth)
+            term = dot(xn[kk, b, :, columns], gl[kk, yy, :, lanes])
+            value = term if value is None else value + term
+        return value, lanes
+
+    def inputs(kk, first, yys):
         @pl.loop(0, zs * tiles)
         def _(i):
             b, n = i // tiles, i % tiles
-            value, lanes = product(kk, b, n)
+            value, lanes = product(kk, b, n, yys)
             if first:
                 acc[b, :, lanes] = value
             else:
                 acc[b, :, lanes] = acc[b, :, lanes] + value
 
-    inputs(0, True)
-    g_took(2, 1)
-    inputs(1, False)
-    g_took(3, 0)
-    g_took(3, 1)
-    inputs(2, False)
+    def gl_whole(zz):
+        for i in range(2):
+            arrived(gl_at(zz, 1 - y, i), g_y.at[zz, i])
+
+    for b in range(zs):
+        for k in (ccol, dcol):
+            arrived(xn.at[k, b], t_r.at[k, b])
+    gl_whole(z)
+    inputs(z, True, (0, 1))
+    stage(2)
+    both(lambda: g_took(last, 1), lambda: g_took(third, 0))
+    gl_whole(near[1])
+    inputs(near[1], False, (0, 1))
+    stage(3)
+
+    def on_outer():
+        g_took(third, 1)
+        g_took(last, 0)
+
+    pl.when(outer)(on_outer)
+    gl_whole(third)
+    inputs(third, False, (0, 1))
+    stage(4)
+    w_stage(0)
+    pl.when(outer)(lambda: g_took(last, 1))
+    inputs(last, False, (y,))
 
     orders = [sorted(range(zs), key=lambda b, at=at: -abs(b - at)) for at in range(zs)]
     blocks = [pick(z, [order[j] for order in orders]) for j in range(zs)]
 
-    last = near[3]
-    for i in range(2):
-        arrived(gl_at(last, 1 - y, i), g_y.at[last, i])
+    gl_whole(last)
     cut = 64
+
+    def h_send(j):
+        b = blocks[j]
+        copy(hid_at(b, col), hid_at(b, col), h_x.at[j], h_r.at[col, b], at_x).start()
+        copy(hid_at(b, col), hid_at(b, col), h_c.at[j], h_r.at[col, b], at_c).start()
 
     for j in range(zs):
         b = blocks[j]
 
         @pl.loop(0, tiles)
         def _(n, b=b):
-            value, lanes = product(last, b, n)
+            value, lanes = product(last, b, n, (1 - y,))
             acc[b, :, lanes] = acc[b, :, lanes] + value
 
         @pl.loop(0, size // cut)
@@ -294,8 +353,8 @@
             value = (jax.nn.gelu(gate, approximate=True) * linear).astype(BF16)
             hid[b, rows, pl.ds(pl.multiple_of(col * part, 128), part)] = value
 
-        copy(hid_at(b, col), hid_at(b, col), h_x.at[j], h_r.at[col, b], at_x).start()
-        copy(hid_at(b, col), hid_at(b, col), h_c.at[j], h_r.at[col, b], at_c).start()
+        if j < 2:
+            h_send(j)
 
     def h_over(j):
         b = blocks[j]
@@ -323,86 +382,124 @@
     def _():
         pl.semaphore_signal(credit.at[1], inc=1, device_id=at_z(z + 1), device_id_type=MESH)
 
+    def outputs(h, j):
+        b = blocks[j]
+
+        @pl.loop(0, 2)
+        def _(yy):
+            value = dot(hid[b], wo[yy, :, pl.ds(h * wide, wide)])
+            acc[b, :, pl.ds(pl.multiple_of(h * outw + yy * wide, wide), wide)] = value
+
+    def half_of(slot, b, h):
+        return xn.at[slot, b, :, pl.ds(h * outw, outw)]
+
+    def carries(h, b):
+        from_left = (b >= z) & (z > 0)
+        from_right = (b <= z) & (z < zs - 1)
+        slot = jnp.where(b == z, 2, 0)
+        pl.when(from_left)(lambda: arrived(half_of(0, b, h), o_r.at[0, b, h]))
+        pl.when(from_right)(lambda: arrived(half_of(slot, b, h), o_r.at[1, b, h]))
+        return from_left, from_right
+
+    def relay(h, j):
+        b = blocks[j]
+        from_left, from_right = carries(h, b)
+        lanes = pl.ds(h * outw, outw)
+        carry = from_left | from_right
+
+        @pl.loop(0, size // cut)
+        def _(i):
+            rows = pl.ds(pl.multiple_of(i * cut, cut), cut)
+            value = acc[b, rows, lanes] + jnp.where(carry, xn[0, b, rows, lanes].astype(F32), 0.0)
+            xn[1, b, rows, lanes] = value.astype(BF16)
+
+        @pl.when(b > z)
+        def _():
+            copy(half_of(1, b, h), half_of(0, b, h), o_s.at[j, h], o_r.at[0, b, h], at_z(z + 1)).start()
+
+        @pl.when(b < z)
+        def _():
+            slot = jnp.where(b == z - 1, 2, 0)
+            copy(half_of(1, b, h), half_of(slot, b, h), o_s.at[j, h], o_r.at[1, b, h], at_z(z - 1)).start()
+
+    def finish(h):
+        from_left, from_right = carries(h, z)
+
+        @pl.loop(0, size // cut)
+        def _(i):
+            rows = pl.ds(pl.multiple_of(i * cut, cut), cut)
+            for yy in range(2):
+                lanes = pl.ds(h * outw + yy * wide, wide)
+                value = acc[z, rows, lanes]
+                value = value + jnp.where(from_left, xn[0, z, rows, lanes].astype(F32), 0.0)
+                value = value + jnp.where(from_right, xn[2, z, rows, lanes].astype(F32), 0.0)
+                out[rows, pl.ds(yy * outw + h * wide, wide)] = value.astype(BF16)
+
+    def hid_whole(j):
+        for k in (ccol, dcol):
+            arrived(hid_at(blocks[j], k), h_r.at[k, blocks[j]])
+
+    def wo_whole(h):
+        for p in range(zs):
+            arrived(wo_at(1 - y, p, h), w_y.at[p, h])
+
+    w_stage(1)
+    for m in range(1, zs):
+        w_took(m, 0)
+    h_send(2)
     h_over(0)
-    w_took(2)
-    w_took(3)
+    for p in (ccol, xcol, dcol):
+        w_over(p, 0)
     h_over(1)
-    w_took(1)
-
-    def w_over(p):
-        arrived(wo_at(y, p), w_x.at[p])
-        copy(wo_at(y, p), wo_at(y, p), w_ys.at[p], w_y.at[p], at_y).start()
-
-    w_over(ccol)
-    w_over(xcol)
-    w_over(dcol)
+    wo_whole(0)
+    hid_whole(0)
+    outputs(0, 0)
     pl.when(z < zs - 1)(lambda: pl.semaphore_wait(credit.at[0], 1))
     pl.when(z > 0)(lambda: pl.semaphore_wait(credit.at[1], 1))
+    relay(0, 0)
+    hid_whole(1)
+    outputs(0, 1)
+    relay(0, 1)
+    for m in range(1, zs):
+        w_took(m, 1)
+    h_send(3)
     h_over(2)
+    for p in (ccol, xcol, dcol):
+        w_over(p, 1)
+    hid_whole(2)
+    outputs(0, 2)
+    relay(0, 2)
+    wo_whole(1)
+    for j in range(zs - 1):
+        outputs(1, j)
+        relay(1, j)
     h_over(3)
-    for p in range(zs):
-        arrived(wo_at(1 - y, p), w_y.at[p])
-
-    wide = 2 * LANES
-    half = outw // wide
-    for j in range(zs):
-        b = blocks[j]
-        for k in (ccol, dcol):
-            arrived(hid_at(b, k), h_r.at[k, b])
-        from_left = (b >= z) & (z > 0)
-        from_right = (b <= z) & (z < zs - 1)
-
-        @pl.when(from_left)
-        def _(b=b):
-            arrived(xn.at[0, b], o_r.at[0, b])
-
-        @pl.when(from_right)
-        def _(b=b):
-            slot = jnp.where(b == z, 2, 0)
-            arrived(xn.at[slot, b], o_r.at[1, b])
-
-        @pl.loop(0, 2 * half)
-        def _(n, b=b, j=j, from_left=from_left, from_right=from_right):
-            yy, at = n // half, n % half
-            value = dot(hid[b], wo[yy, :, pl.ds(pl.multiple_of(at * wide, wide), wide)])
-            lanes = pl.ds(pl.multiple_of(n * wide, wide), wide)
-            if j < zs - 1:
-                carried = xn[0, b, :, lanes].astype(F32)
-                value = value + jnp.where(from_left | from_right, carried, 0.0)
-                xn[1, b, :, lanes] = value.astype(BF16)
-            else:
-                value = value + jnp.where(from_left, xn[0, b, :, lanes].astype(F32), 0.0)
-                value = value + jnp.where(from_right, xn[2, b, :, lanes].astype(F32), 0.0)
-                out[:, lanes] = value.astype(BF16)
-
-        if j < zs - 1:
-
-            @pl.when(b > z)
-            def _(b=b, j=j):
-                copy(xn.at[1, b], xn.at[0, b], o_s.at[j], o_r.at[0, b], at_z(z + 1)).start()
-
-            @pl.when(b < z)
-            def _(b=b, j=j):
-                slot = jnp.where(b == z - 1, 2, 0)
-                copy(xn.at[1, b], xn.at[slot, b], o_s.at[j], o_r.at[1, b], at_z(z - 1)).start()
+    hid_whole(3)
+    for h in range(2):
+        outputs(h, zs - 1)
+    for h in range(2):
+        finish(h)
 
     for n in range(3):
         left_here(ss.at[col], ss_s.at[n])
+    pl.when(inner)(lambda: left_here(gl_at(z, y, 0), g_zs.at[2, 0]))
     for m in range(zs):
         for i in range(2):
-            if m:
+            if m == 1:
                 left_here(gl_at(z, y, i), g_zs.at[m, i])
-            left_here(gl_at(near[m], y, i), g_ys.at[m, i])
-        if m:
-            left_here(wo_at(w_slab, w_block), w_zs.at[m])
-        pl.when(near[m] != col)(lambda m=m: left_here(wo_at(y, col), w_xs.at[m]))
-        left_here(wo_at(y, m), w_ys.at[m])
+            left_here(gl_at(m, y, i), g_ys.at[m, i])
+        for h in range(2):
+            if m == 1 or m and h:
+                left_here(wo_at(w_slab, w_block, h), w_zs.at[m, h])
+            pl.when(near[m] != col)(lambda m=m, h=h: left_here(wo_at(y, col, h), w_xs.at[m, h]))
+            left_here(wo_at(y, m, h), w_ys.at[m, h])
     for j in range(zs):
         left_here(hid_at(blocks[j], col), h_x.at[j])
         left_here(hid_at(blocks[j], col), h_c.at[j])
         left_here(hid_at(blocks[j], xcol), h_d.at[j])
         if j < zs - 1:
-            left_here(xn.at[1, blocks[j]], o_s.at[j])
+            for h in range(2):
+                left_here(half_of(1, blocks[j], h), o_s.at[j, h])
 
 
 def scratch_of(zs, size, width, depth, part, outw):
@@ -417,8 +514,8 @@
         ((cols, size, LANES), F32),
     ]
     sems = [
-        (4,), (3,), (cols,), (cols, zs), (zs,), (zs,), (zs,), (zs,), (zs,), (zs, 2), (zs, 2), (zs, 2), (zs, 2),
-        (zs,), (zs,), (cols,), (zs,), (cols,), (cols,), (cols, zs), (zs,), (zs,), (zs,), (2, zs), (zs,),
+        (5,), (3,), (cols,), (cols, zs), (zs,), (zs,), (zs,), (zs,), (zs,), (zs, 2), (zs, 2), (zs, 2), (zs, 2),
+        (zs, 2), (zs, 2), (cols, 2), (zs, 2), (cols, 2), (cols, 2), (cols, zs), (zs,), (zs,), (zs,), (2, zs, 2), (zs, 2),
     ]
     return buffers, [dma(s) for s in sems] + [pltpu.SemaphoreType.REGULAR((2,))]
 

time: 408 us -> 355 us (0.87)
  Pallas kernels: 404 us -> 349 us
    pallas_call x1, Pallas kernels: 404 us -> 349 us  [fused(): pl.pallas_call(functools.partial(body, zs), out_shape=jax.ShapeDtypeStruc...]
where the time goes in v1:
time: 355 us; the launch traced here: 352 us
  Pallas kernels  349 us (98%)
    pallas_call x1, Pallas kernels, fused(): pl.pallas_call(functools.partial(body, zs), out_shape=jax.ShapeDtypeStruc...  349 us

profile of v1, /device:TPU:20, one launch (start us, length us, event | category | flops | bytes accessed | tf_op | source)
XLA Modules:
  0.0 352.5 jit_solution(13988009852956221654)
XLA Ops:
  0.0 1.3 reshape.3.gain
  1.3 348.9 %ffn.1 = bf16[512,1024]{1,0:T(8,128)(2,1)} custom-call(bf16[512,1024]{1,0:T(8,128)(2,1)} %tokens.1, bf16[1,1024]{1,0:T(2,128)(2,1)} %reshape.3.gain, bf16[512,2560]{1,0:T(8,128)(2,1)} %gate_w.1, bf16[512,2560]{1,0:T(8,128)(2,1)} %linear_w.1, bf16[2560,512]{1,0:T(8,128)(2,1)} %out_w.1), custom_call_target="tpu_custom_call" | custom-call | tf_op jit(solution)/shard_map/ffn/pallas_call | solution.py:526
  350.2 2.3 copy.7

commit v2 on v1

--- a/solution.py
+++ b/solution.py
@@ -51,6 +51,9 @@
     outw = out_w.shape[1]
     features = width * zs
     wide = outw // 2
+    first_share = (part // LANES + 1) // 2 * LANES
+    shares = (first_share, part - first_share)
+    starts = (0, 2 * first_share)
     row, col = lax.axis_index("row"), lax.axis_index("col")
     z, y = row // 2, row % 2
     x, core = col // 2, col % 2
@@ -78,7 +81,10 @@
         copy(ref, ref, sem, sem, at_c).wait_send()
 
     def gl_at(zz, yy, i):
-        return gl.at[zz, yy, :, pl.ds(i * part, part)]
+        return gl.at[zz, yy, :, pl.ds(starts[i], 2 * shares[i])]
+
+    def gl_of(zz, yy, i, which):
+        return gl.at[zz, yy, :, pl.ds(starts[i] + which * shares[i], shares[i])]
 
     def wo_at(slab, block, h):
         rows = pl.ds(pl.multiple_of(block * part, 128), part)
@@ -87,20 +93,23 @@
     def out_rows(to, h):
         return out_w.at[pl.ds(pl.multiple_of(to * part, 128), part), pl.ds(h * wide, wide)]
 
-    def hid_at(b, k):
-        return hid.at[b, :, pl.ds(pl.multiple_of(k * part, 128), part)]
-
-    def cols_of(w, to):
-        return w.at[:, pl.ds(pl.multiple_of(to * part, 128), part)]
+    def hid_at(b, k, i):
+        return hid.at[b, :, pl.ds(pl.multiple_of(k * part + i * first_share, LANES), shares[i])]
+
+    def cols_of(w, to, i):
+        return w.at[:, pl.ds(pl.multiple_of(to * part + i * first_share, LANES), shares[i])]
 
     own = xn.at[col, z]
     w_slab, w_block = jnp.where(z == col, y, 2), jnp.where(z == col, col, z)
     ins = [
         pltpu.make_async_copy(tokens, own, loc.at[0]),
-        pltpu.make_async_copy(cols_of(gate_w, z), gl_at(z, y, 0), loc.at[1]),
-        pltpu.make_async_copy(cols_of(linear_w, z), gl_at(z, y, 1), loc.at[2]),
-        pltpu.make_async_copy(out_rows(z, 0), wo_at(w_slab, w_block, 0), loc.at[3]),
-        pltpu.make_async_copy(out_rows(z, 1), wo_at(w_slab, w_block, 1), loc.at[4]),
+        pltpu.make_async_copy(out_rows(z, 0), wo_at(w_slab, w_block, 0), loc.at[1]),
+        pltpu.make_async_copy(out_rows(z, 1), wo_at(w_slab, w_block, 1), loc.at[2]),
+    ]
+    ins += [
+        pltpu.make_async_copy(cols_of(w, z, i), gl_of(z, y, i, which), loc.at[3 + 2 * i + which])
+        for i in range(2)
+        for which, w in enumerate((gate_w, linear_w))
     ]
     for each in ins:
         each.start()
@@ -124,9 +133,10 @@
 
     def g_send(m, i):
         to = near[m]
-        copy(
-            cols_of((gate_w, linear_w)[i], to), gl_at(z, y, i), g_zs.at[m, i], g_z.at[z, i], at_z(to)
-        ).start()
+        for which, w in enumerate((gate_w, linear_w)):
+            copy(
+                cols_of(w, to, i), gl_of(z, y, i, which), g_zs.at[m, i], g_z.at[z, i], at_z(to)
+            ).start()
 
     def g_pass(zz, i):
         ref = gl_at(zz, y, i)
@@ -140,10 +150,10 @@
     pl.when(inner)(lambda: g_send(2, 0))
     for n, peer in enumerate((at_x, at_c, at_d)):
         copy(ss.at[col], ss.at[col], ss_s.at[n], ss_r.at[col], peer).start()
-    ins[1].wait()
-    g_pass(z, 0)
-    ins[2].wait()
-    g_pass(z, 1)
+    for i in range(2):
+        for which in range(2):
+            ins[3 + 2 * i + which].wait()
+        g_pass(z, i)
     for k in (xcol, ccol, dcol):
         arrived(ss.at[k], ss_r.at[k])
 
@@ -200,38 +210,43 @@
         copy(wo_at(y, p, h), wo_at(y, p, h), w_ys.at[p, h], w_y.at[p, h], at_y).start()
 
     def t_step(s):
-        @pl.when(z >= s)
-        def _():
-            b = z - s
-            arrived(xn.at[col, b], t_r.at[col, b])
-            pl.when(z < zs - 1)(lambda: t_right(b))
-            t_col(b)
-
-        @pl.when(z + s < zs)
-        def _():
-            b = z + s
-            arrived(xn.at[col, b], t_r.at[col, b])
-            pl.when(z > 0)(lambda: t_left(b))
-            t_col(b)
+        below, above = z >= s, z + s < zs
+
+        def from_below():
+            arrived(xn.at[col, z - s], t_r.at[col, z - s])
+            pl.when(z < zs - 1)(lambda: t_right(z - s))
+
+        def from_above():
+            arrived(xn.at[col, z + s], t_r.at[col, z + s])
+            pl.when(z > 0)(lambda: t_left(z + s))
+
+        pl.when(below & (z < zs // 2))(from_below)
+        pl.when(above)(from_above)
+        pl.when(below & (z >= zs // 2))(from_below)
+        pl.when(below)(lambda: t_col(z - s))
+        pl.when(above)(lambda: t_col(z + s))
 
     def t_over_step(s):
         pl.when(z >= s)(lambda: t_over(z - s))
         pl.when(z + s < zs)(lambda: t_over(z + s))
 
-    far_inner, far_outer = ((2, 1), (3, 0), (3, 1)), ((3, 0), (3, 1), (2, 0), (2, 1))
+    far_outer = ((3, 0), (2, 0), (3, 1), (2, 1))
 
     def both(on_inner, on_outer):
         pl.when(inner)(on_inner)
         pl.when(outer)(on_outer)
 
-    def stage(k):
-        def on(pieces):
-            if 0 < k <= len(pieces):
-                left_here(gl_at(z, y, 0), g_zs.at[pieces[k - 1]])
-            if k < len(pieces):
-                g_send(*pieces[k])
-
-        both(lambda: on(far_inner), lambda: on(far_outer))
+    def stage(k, pieces):
+        if 0 < k <= len(pieces):
+            m, i = pieces[k - 1]
+            left_here(gl_at(z, y, i), g_zs.at[m, i])
+        for n in (0, 1) if k == 0 else (k + 1,):
+            if n < len(pieces):
+                g_send(*pieces[n])
+
+    def near_out():
+        for h in range(2):
+            w_send(1, h)
 
     def w_stage(h):
         if h:
@@ -242,7 +257,7 @@
             for m in order:
                 w_send(m, h)
 
-        both(lambda: on((2, 3)), lambda: on((3, 2)))
+        both(lambda: on((2, 3) if h else (3,)), lambda: on((3, 2)))
 
     pl.when(z < zs - 1)(lambda: t_right(z))
     pl.when(z > 0)(lambda: t_left(z))
@@ -251,29 +266,51 @@
     third = jnp.where(inner, near[2], near[3])
     last = jnp.where(inner, near[3], near[2])
     g_took(near[1], 0)
-    pl.when(inner)(lambda: g_took(third, 0))
     t_step(1)
 
-    pl.when(inner)(lambda: g_took(near[1], 1))
+    def early():
+        g_took(third, 0)
+        g_took(near[1], 1)
+
+    pl.when(inner)(early)
     t_step(2)
-    stage(0)
-    pl.when(inner)(lambda: g_send(1, 1))
+
+    def relayed(up, b):
+        left_here(xn.at[col, b], (t_zr if up else t_zl).at[b])
+
+    lower, upper = inner & (z < zs // 2), inner & (z >= zs // 2)
+    pl.when(lower)(lambda: relayed(True, z - 1))
+    pl.when(upper)(lambda: relayed(False, z + 1))
+    @pl.when(inner)
+    def _():
+        g_send(2, 1)
+        w_send(2, 0)
+
     t_step(3)
+    pl.when(outer)(lambda: stage(0, far_outer))
     t_over(z)
     t_over_step(1)
-    stage(1)
-    for h in range(2):
-        w_send(1, h)
-
-    def on_inner():
+
+    @pl.when(lower)
+    def _():
+        relayed(False, z + 1)
+        relayed(False, z + 2)
+
+    @pl.when(upper)
+    def _():
+        relayed(True, z - 1)
+        relayed(True, z - 2)
+
+    @pl.when(inner)
+    def _():
+        g_send(1, 1)
+        g_send(3, 0)
         g_took(third, 1)
-        g_took(last, 0)
-
-    both(on_inner, lambda: g_took(near[1], 1))
+
     t_over_step(2)
     t_over_step(3)
     for h in range(2):
-        ins[3 + h].wait()
+        ins[1 + h].wait()
         w_out(0, h)
 
     tile = 2 * LANES
@@ -289,88 +326,116 @@
             value = term if value is None else value + term
         return value, lanes
 
-    def inputs(kk, first, yys):
-        @pl.loop(0, zs * tiles)
-        def _(i):
-            b, n = i // tiles, i % tiles
-            value, lanes = product(kk, b, n, yys)
+    def inputs(kk, i, first, yys, block=None):
+        count = 2 * shares[i] // tile
+
+        @pl.loop(0, count if block is not None else zs * count)
+        def _(n):
+            b, at = (n // count, n % count) if block is None else (block, n)
+            value, lanes = product(kk, b, starts[i] // tile + at, yys)
             if first:
                 acc[b, :, lanes] = value
             else:
                 acc[b, :, lanes] = acc[b, :, lanes] + value
 
-    def gl_whole(zz):
-        for i in range(2):
-            arrived(gl_at(zz, 1 - y, i), g_y.at[zz, i])
+    def gl_whole(zz, i):
+        arrived(gl_at(zz, 1 - y, i), g_y.at[zz, i])
+
+    cut = 64
+
+    def h_send(j, i):
+        b = blocks[j]
+        copy(hid_at(b, col, i), hid_at(b, col, i), h_x.at[j, i], h_r.at[col, b, i], at_x).start()
+        copy(hid_at(b, col, i), hid_at(b, col, i), h_c.at[j, i], h_r.at[col, b, i], at_c).start()
+
+    def h_over(j, i):
+        b = blocks[j]
+        arrived(hid_at(b, xcol, i), h_r.at[xcol, b, i])
+        copy(hid_at(b, xcol, i), hid_at(b, xcol, i), h_d.at[j, i], h_r.at[xcol, b, i], at_c).start()
+
+    def hidden(j, i):
+        b = blocks[j]
+
+        @pl.loop(0, size // cut)
+        def _(n):
+            rows = pl.ds(pl.multiple_of(n * cut, cut), cut)
+            gate = acc[b, rows, pl.ds(starts[i], shares[i])]
+            linear = acc[b, rows, pl.ds(starts[i] + shares[i], shares[i])]
+            value = (jax.nn.gelu(gate, approximate=True) * linear).astype(BF16)
+            hid[b, rows, pl.ds(pl.multiple_of(col * part + i * first_share, LANES), shares[i])] = value
+
+    orders = [sorted(range(zs), key=lambda b, at=at: -abs(b - at)) for at in range(zs)]
+    blocks = [pick(z, [order[j] for order in orders]) for j in range(zs)]
 
     for b in range(zs):
         for k in (ccol, dcol):
             arrived(xn.at[k, b], t_r.at[k, b])
-    gl_whole(z)
-    inputs(z, True, (0, 1))
-    stage(2)
-    both(lambda: g_took(last, 1), lambda: g_took(third, 0))
-    gl_whole(near[1])
-    inputs(near[1], False, (0, 1))
-    stage(3)
-
-    def on_outer():
-        g_took(third, 1)
+    gl_whole(z, 0)
+    inputs(z, 0, True, (0, 1))
+
+    @pl.when(inner)
+    def _():
+        g_send(3, 1)
         g_took(last, 0)
 
-    pl.when(outer)(on_outer)
-    gl_whole(third)
-    inputs(third, False, (0, 1))
-    stage(4)
+    pl.when(outer)(lambda: stage(1, far_outer))
+    near_out()
+    gl_whole(near[1], 0)
+    inputs(near[1], 0, False, (0, 1))
+
+    @pl.when(outer)
+    def _():
+        g_took(near[1], 1)
+        g_took(third, 0)
+
+    gl_whole(z, 1)
+    inputs(z, 1, True, (0, 1))
+
+    @pl.when(outer)
+    def _():
+        stage(2, far_outer)
+        g_took(last, 0)
+
+    gl_whole(near[1], 1)
+    inputs(near[1], 1, False, (0, 1))
+    gl_whole(third, 0)
+    inputs(third, 0, False, (0, 1))
+    pl.when(outer)(lambda: g_took(third, 1))
+    gl_whole(last, 0)
+    for j in range(zs):
+        inputs(last, 0, False, (0, 1), blocks[j])
+        hidden(j, 0)
+        h_send(j, 0)
+    pl.when(outer)(lambda: stage(3, far_outer))
+    pl.when(inner)(lambda: g_took(last, 1))
+    gl_whole(third, 1)
+    inputs(third, 1, False, (0, 1))
+
+    def inner_left():
+        for m, i in ((2, 1), (3, 0), (3, 1)):
+            left_here(gl_at(z, y, i), g_zs.at[m, i])
+
+    both(inner_left, lambda: stage(4, far_outer))
     w_stage(0)
     pl.when(outer)(lambda: g_took(last, 1))
-    inputs(last, False, (y,))
-
-    orders = [sorted(range(zs), key=lambda b, at=at: -abs(b - at)) for at in range(zs)]
-    blocks = [pick(z, [order[j] for order in orders]) for j in range(zs)]
-
-    gl_whole(last)
-    cut = 64
-
-    def h_send(j):
-        b = blocks[j]
-        copy(hid_at(b, col), hid_at(b, col), h_x.at[j], h_r.at[col, b], at_x).start()
-        copy(hid_at(b, col), hid_at(b, col), h_c.at[j], h_r.at[col, b], at_c).start()
-
+    inputs(last, 1, False, (y,))
+    gl_whole(last, 1)
     for j in range(zs):
-        b = blocks[j]
-
-        @pl.loop(0, tiles)
-        def _(n, b=b):
-            value, lanes = product(last, b, n, (1 - y,))
-            acc[b, :, lanes] = acc[b, :, lanes] + value
-
-        @pl.loop(0, size // cut)
-        def _(i, b=b):
-            rows = pl.ds(pl.multiple_of(i * cut, cut), cut)
-            gate = acc[b, rows, :part]
-            linear = acc[b, rows, part:]
-            value = (jax.nn.gelu(gate, approximate=True) * linear).astype(BF16)
-            hid[b, rows, pl.ds(pl.multiple_of(col * part, 128), part)] = value
-
+        inputs(last, 1, False, (1 - y,), blocks[j])
+        hidden(j, 1)
         if j < 2:
-            h_send(j)
-
-    def h_over(j):
-        b = blocks[j]
-        arrived(hid_at(b, xcol), h_r.at[xcol, b])
-        copy(hid_at(b, xcol), hid_at(b, xcol), h_d.at[j], h_r.at[xcol, b], at_c).start()
+            h_send(j, 1)
 
     for b in range(zs):
         left_here(xn.at[col, b], t_x.at[b])
         left_here(xn.at[col, b], t_c.at[b])
         left_here(xn.at[xcol, b], t_d.at[b])
 
-        @pl.when((b <= z) & (z < zs - 1))
+        @pl.when((b <= z) & (z < zs - 1) & (outer | (b == z)))
         def _(b=b):
             left_here(xn.at[col, b], t_zr.at[b])
 
-        @pl.when((b >= z) & (z > 0))
+        @pl.when((b >= z) & (z > 0) & (outer | (b == z)))
         def _(b=b):
             left_here(xn.at[col, b], t_zl.at[b])
 
@@ -437,43 +502,48 @@
 
     def hid_whole(j):
         for k in (ccol, dcol):
-            arrived(hid_at(blocks[j], k), h_r.at[k, blocks[j]])
+            for i in range(2):
+                arrived(hid_at(blocks[j], k, i), h_r.at[k, blocks[j], i])
 
     def wo_whole(h):
         for p in range(zs):
             arrived(wo_at(1 - y, p, h), w_y.at[p, h])
 
-    w_stage(1)
     for m in range(1, zs):
         w_took(m, 0)
-    h_send(2)
-    h_over(0)
+    h_send(2, 1)
+    h_send(3, 1)
+    w_stage(1)
+    for j in range(zs):
+        h_over(j, 0)
+    h_over(0, 1)
+    h_over(1, 1)
     for p in (ccol, xcol, dcol):
         w_over(p, 0)
-    h_over(1)
     wo_whole(0)
     hid_whole(0)
     outputs(0, 0)
     pl.when(z < zs - 1)(lambda: pl.semaphore_wait(credit.at[0], 1))
     pl.when(z > 0)(lambda: pl.semaphore_wait(credit.at[1], 1))
-    relay(0, 0)
+    pl.when(outer)(lambda: relay(0, 0))
     hid_whole(1)
     outputs(0, 1)
-    relay(0, 1)
+    pl.when(outer)(lambda: relay(0, 1))
     for m in range(1, zs):
         w_took(m, 1)
-    h_send(3)
-    h_over(2)
+    h_over(2, 1)
+    h_over(3, 1)
+    hid_whole(2)
+    outputs(0, 2)
+    both(lambda: relay(0, 0), lambda: relay(0, 2))
     for p in (ccol, xcol, dcol):
         w_over(p, 1)
-    hid_whole(2)
-    outputs(0, 2)
-    relay(0, 2)
+    pl.when(inner)(lambda: relay(0, 1))
+    pl.when(inner)(lambda: relay(0, 2))
     wo_whole(1)
     for j in range(zs - 1):
         outputs(1, j)
         relay(1, j)
-    h_over(3)
     hid_whole(3)
     for h in range(2):
         outputs(h, zs - 1)
@@ -494,9 +564,9 @@
             pl.when(near[m] != col)(lambda m=m, h=h: left_here(wo_at(y, col, h), w_xs.at[m, h]))
             left_here(wo_at(y, m, h), w_ys.at[m, h])
     for j in range(zs):
-        left_here(hid_at(blocks[j], col), h_x.at[j])
-        left_here(hid_at(blocks[j], col), h_c.at[j])
-        left_here(hid_at(blocks[j], xcol), h_d.at[j])
+        for i in range(2):
+            for sem in (h_x, h_c, h_d):
+                left_here(hid_at(blocks[j], col, i), sem.at[j, i])
         if j < zs - 1:
             for h in range(2):
                 left_here(half_of(1, blocks[j], h), o_s.at[j, h])
@@ -514,8 +584,9 @@
         ((cols, size, LANES), F32),
     ]
     sems = [
-        (5,), (3,), (cols,), (cols, zs), (zs,), (zs,), (zs,), (zs,), (zs,), (zs, 2), (zs, 2), (zs, 2), (zs, 2),
-        (zs, 2), (zs, 2), (cols, 2), (zs, 2), (cols, 2), (cols, 2), (cols, zs), (zs,), (zs,), (zs,), (2, zs, 2), (zs, 2),
+        (7,), (3,), (cols,), (cols, zs), (zs,), (zs,), (zs,), (zs,), (zs,), (zs, 2), (zs, 2), (zs, 2), (zs, 2),
+        (zs, 2), (zs, 2), (cols, 2), (zs, 2), (cols, 2), (cols, 2), (cols, zs, 2), (zs, 2), (zs, 2), (zs, 2), (2, zs, 2),
+        (zs, 2),
     ]
     return buffers, [dma(s) for s in sems] + [pltpu.SemaphoreType.REGULAR((2,))]
 

time: 355 us -> 344 us (0.969)
  Pallas kernels: 349 us -> 336 us
    pallas_call x1, Pallas kernels: 349 us -> 336 us  [fused(): pl.pallas_call(functools.partial(body, zs), out_shape=jax.ShapeDtypeStruc...]
where the time goes in v2:
time: 344 us; the launch traced here: 340 us
  Pallas kernels  336 us (98%)
  local copies, waits for them, and re-layouts  3.54 us (1%)
    pallas_call x1, Pallas kernels, fused(): pl.pallas_call(functools.partial(body, zs), out_shape=jax.ShapeDtypeStruc...  336 us

profile of v2, /device:TPU:20, one launch (start us, length us, event | category | flops | bytes accessed | tf_op | source)
XLA Modules:
  0.0 340.0 jit_solution(8844577440688435086)
XLA Ops:
  0.0 1.3 reshape.3.gain
  1.3 336.5 %ffn.1 = bf16[512,1024]{1,0:T(8,128)(2,1)} custom-call(bf16[512,1024]{1,0:T(8,128)(2,1)} %tokens.1, bf16[1,1024]{1,0:T(2,128)(2,1)} %reshape.3.gain, bf16[512,2560]{1,0:T(8,128)(2,1)} %gate_w.1, bf16[512,2560]{1,0:T(8,128)(2,1)} %linear_w.1, bf16[2560,512]{1,0:T(8,128)(2,1)} %out_w.1), custom_call_target="tpu_custom_call" | custom-call | tf_op jit(solution)/shard_map/ffn/pallas_call | solution.py:597
  337.8 2.3 copy.7

commit v3 on v2

--- a/solution.py
+++ b/solution.py
@@ -509,17 +509,19 @@
         for p in range(zs):
             arrived(wo_at(1 - y, p, h), w_y.at[p, h])
 
+    w_stage(1)
     for m in range(1, zs):
         w_took(m, 0)
     h_send(2, 1)
     h_send(3, 1)
-    w_stage(1)
     for j in range(zs):
         h_over(j, 0)
     h_over(0, 1)
     h_over(1, 1)
     for p in (ccol, xcol, dcol):
         w_over(p, 0)
+    for m in range(1, zs):
+        w_took(m, 1)
     wo_whole(0)
     hid_whole(0)
     outputs(0, 0)
@@ -529,15 +531,13 @@
     hid_whole(1)
     outputs(0, 1)
     pl.when(outer)(lambda: relay(0, 1))
-    for m in range(1, zs):
-        w_took(m, 1)
+    for p in (ccol, xcol, dcol):
+        w_over(p, 1)
     h_over(2, 1)
     h_over(3, 1)
     hid_whole(2)
     outputs(0, 2)
     both(lambda: relay(0, 0), lambda: relay(0, 2))
-    for p in (ccol, xcol, dcol):
-        w_over(p, 1)
     pl.when(inner)(lambda: relay(0, 1))
     pl.when(inner)(lambda: relay(0, 2))
     wo_whole(1)

time: 344 us -> 340 us (0.988)
  no operation moved by 1% of the time
where the time goes in v3:
time: 340 us; the launch traced here: 338 us
  Pallas kernels  335 us (99%)
  local copies, waits for them, and re-layouts  3.54 us (1%)
    pallas_call x1, Pallas kernels, fused(): pl.pallas_call(functools.partial(body, zs), out_shape=jax.ShapeDtypeStruc...  335 us

profile of v3, /device:TPU:20, one launch (start us, length us, event | category | flops | bytes accessed | tf_op | source)
XLA Modules:
  0.0 338.3 jit_solution(17666537969482019438)
XLA Ops:
  0.0 1.3 reshape.3.gain
  1.3 334.7 %ffn.1 = bf16[512,1024]{1,0:T(8,128)(2,1)} custom-call(bf16[512,1024]{1,0:T(8,128)(2,1)} %tokens.1, bf16[1,1024]{1,0:T(2,128)(2,1)} %reshape.3.gain, bf16[512,2560]{1,0:T(8,128)(2,1)} %gate_w.1, bf16[512,2560]{1,0:T(8,128)(2,1)} %linear_w.1, bf16[2560,512]{1,0:T(8,128)(2,1)} %out_w.1), custom_call_target="tpu_custom_call" | custom-call | tf_op jit(solution)/shard_map/ffn/pallas_call | solution.py:597
  336.0 2.3 copy.7
